TPU v7x, 32 devices: a whole 2x2x4 slice. The times are simulated.
32 devices in a mesh: lon: 4 (over y, x), lat: 8 (over z, core).
Axes of the slice: x: 2, y: 2, z: 4, core: 2. Of those that a mesh axis runs over, the one named last changes fastest.
Arguments:
- meridional_speed: float32 [16, 512, 1024], P(None, 'lat', 'lon'), may hold values from -6 to 6
- theta_field: float32 [16, 512, 1024], P(None, 'lat', 'lon'), may hold values from -2 to 30
- tier_vertical_span: float32 [16], replicated, may hold values from 0.5 to 4
- grid_zonal_span: float32 [512, 1024], P('lat', 'lon'), may hold values from 0.05 to 40
- grid_plan_extent: float32 [512, 1024], P('lat', 'lon'), may hold values from 0.2 to 5
- ocean_energy_input: float32 [512, 1024], P('lat', 'lon'), may hold values from -6 to 6
- ocean_tier_tally: int32 [512, 1024], P('lat', 'lon'), may hold values from 0 to 16, as said below
- grid_region_label: int32 [512, 1024], P('lat', 'lon'), may hold values from 0 to 3
- seam_matching_meridian: int32 [1024], P('lon'), may hold values from 0 to 1023, as said below
Outputs:
- class_transport: float32 [4, 512, 128], P(None, 'lat')
- overturning: float32 [4, 512, 16], P(None, 'lat')
- heat_transport: float32 [4, 512], P(None, 'lat')
- implied_transport: float32 [4, 512], P(None, 'lat')
Inputs may be any that keep to these rules, and one draw needn't show every extreme that they name: `ocean_tier_tally`: one column, the same at every latitude, has at least one wet level, and every column of the northernmost row has at least one. seam_matching_meridian[i] = (c - i) mod 1024 for a c that each draw picks.
All inputs are finite; a program needn't handle non-finite values.
Results may differ from a plain program's by a relative error of at most 0.0003.
Values sent between devices are 32-bit elements; how exact they have to be, the bound alone decides.
A program may use at most 64 MiB of HBM per device.

v0:
```python
import functools
import math

import jax
import jax.numpy as jnp
from jax import lax
from jax.experimental import pallas as pl
from jax.experimental.pallas import tpu as pltpu
from jax.sharding import PartitionSpec as P

THERMAL_BINS = 128
OCEAN_REGIONS = 4
THERMAL_FLOOR = -2.0
THERMAL_RANGE = 32.0

ROWS = 8
DIGIT = 15
HIGHS = -(-(THERMAL_BINS - 1) // DIGIT)
GROUP = 4
STRIDE = 32
MESH = pl.DeviceIdType.MESH
NT = (((1,), (1,)), ((), ()))
HIGHEST = lax.Precision.HIGHEST
BF = jnp.bfloat16
F32 = jnp.float32


def iota(shape, dim):
    return lax.broadcasted_iota(jnp.int32, shape, dim)


def two_parts(x):
    high = x.astype(BF).astype(F32)
    return jnp.concatenate([high, x - high], axis=0).astype(BF)


def exact_parts(x):
    high = x.astype(BF).astype(F32)
    rest = x - high
    mid = rest.astype(BF).astype(F32)
    return jnp.concatenate([high.astype(BF), mid.astype(BF), (rest - mid).astype(BF)], axis=0)


def kernel(
    nlon, nlat, width_total, height_total,
    dz, speed_h, theta_h, dx_h, area_h, flux_h, depth_h, region_h, seam,
    raw,
    speed_v, theta_v, dx_v, area_v, flux_v, depth_v, region_v,
    edge, edge_in, top, top_in, fx, fx_in, total, total_in, buf, got,
    big_sem, small_sem, edge_sem, top_send, top_recv, fx_send, fx_recv, tot_send, tot_recv,
    sum_send, sum_recv,
):
    tiers, blocks, _, width = theta_h.shape
    height = blocks * ROWS
    mylon, mylat = lax.axis_index("lon"), lax.axis_index("lat")
    implied_scale = 2.0 / math.sqrt(width_total * height_total)
    last = blocks - 1

    barrier = pltpu.get_barrier_semaphore()
    for step in range(1, nlon):
        peer = lax.rem(mylon + step, nlon)
        pl.semaphore_signal(barrier, inc=1, device_id=(peer, mylat), device_id_type=MESH)
    for step in range(1, nlat):
        peer = lax.rem(mylat + step, nlat)
        pl.semaphore_signal(barrier, inc=1, device_id=(mylon, peer), device_id_type=MESH)

    small = [
        pltpu.make_async_copy(src, dst, small_sem.at[n])
        for n, (src, dst) in enumerate(
            [
                (area_h, area_v),
                (flux_h, flux_v),
                (region_h, region_v),
                (depth_h, depth_v.at[pl.ds(0, blocks)]),
                (dx_h, dx_v),
            ]
        )
    ]

    def theta_copy(b):
        return pltpu.make_async_copy(theta_h.at[:, b], theta_v.at[b], big_sem.at[0, b])

    def speed_copy(b):
        return pltpu.make_async_copy(speed_h.at[:, b], speed_v.at[b], big_sem.at[1, b])

    for copy in small:
        copy.start()
    theta_copy(0).start()
    theta_copy(last).start()
    for b in range(blocks):
        speed_copy(b).start()
        if b + 1 < last:
            theta_copy(b + 1).start()
    for copy in small:
        copy.wait()

    region_all = region_v[...].reshape(height, width)
    product = flux_v[...].reshape(height, width) * area_v[...].reshape(height, width)
    fx_rows = jnp.zeros((ROWS, height), F32)
    for b in range(OCEAN_REGIONS):
        part = lax.dot_general(
            jnp.ones((ROWS, width), F32),
            jnp.where(region_all == b, product, 0.0),
            NT, precision=HIGHEST, preferred_element_type=F32,
        )
        fx_rows = jnp.where(iota((ROWS, height), 0) == b, part, fx_rows)
    fx[...] = jnp.zeros_like(fx)
    fx[:, pl.ds(0, height)] = fx_rows

    theta_copy(0).wait()
    theta_copy(last).wait()
    edge[...] = jnp.zeros_like(edge)
    top[...] = jnp.zeros_like(top)
    for k in range(tiers):
        edge[pl.ds(k, 1), :] = theta_v[0, k, pl.ds(0, 1), :]
        top[pl.ds(k, 1), :] = theta_v[last, k, pl.ds(ROWS - 1, 1), :]
    edge[pl.ds(tiers, 1), :] = depth_v[0, pl.ds(0, 1), :].astype(F32)
    top[pl.ds(tiers, 1), :] = depth_v[last, pl.ds(ROWS - 1, 1), :].astype(F32)

    pl.semaphore_wait(barrier, nlon - 1 + nlat - 1)

    edge_copy = pltpu.make_async_remote_copy(
        edge, edge_in, edge_sem.at[0], edge_sem.at[1],
        device_id=(mylon, lax.rem(mylat + nlat - 1, nlat)), device_id_type=MESH,
    )

    def to_lon(src, dst, send, recv, step):
        return pltpu.make_async_remote_copy(
            src, dst.at[step - 1], send.at[step - 1], recv.at[step - 1],
            device_id=(lax.rem(mylon + step, nlon), mylat), device_id_type=MESH,
        )

    def to_lat(step):
        return pltpu.make_async_remote_copy(
            total, total_in.at[step - 1], tot_send.at[step - 1], tot_recv.at[step - 1],
            device_id=(mylon, lax.rem(mylat + step, nlat)), device_id_type=MESH,
        )

    edge_copy.start()
    for step in range(1, nlon):
        to_lon(fx, fx_in, fx_send, fx_recv, step).start()

    @pl.when(mylat == nlat - 1)
    def _():
        for step in range(1, nlon):
            to_lon(top, top_in, top_send, top_recv, step).start()

    def across(offset):
        peer = mylon
        for bit in range(nlon.bit_length() - 1):
            stride = 1 << bit
            if offset & stride:
                peer = peer + stride * (1 - 2 * lax.rem(lax.div(mylon, stride), 2))
        return peer

    def share(offset, src, dst):
        return pltpu.make_async_remote_copy(
            src, dst, sum_send.at[offset - 1], sum_recv.at[offset - 1],
            device_id=(across(offset), mylat), device_id_type=MESH,
        )

    def tree(parts):
        while len(parts) > 1:
            parts = [parts[n] + parts[n + 1] for n in range(0, len(parts), 2)]
        return parts[0]

    def compute(jb):
        reg = region_v[jb].astype(F32)
        dx = dx_v[jb]
        deep = depth_v[jb]
        wet = jnp.minimum(
            deep, jnp.concatenate([deep[1:], depth_v[jb + 1][:1]], axis=0)
        )
        one, zero = jnp.ones((2 * ROWS, width), BF), jnp.zeros((2 * ROWS, width), BF)
        heat = jnp.zeros((ROWS, width), F32)
        warm = jnp.zeros((ROWS, width), F32)
        water = jnp.zeros((ROWS, width), F32)
        levels = []
        acc = None
        for first in range(0, tiers, GROUP):
            lefts, rights = [], []
            for k in range(first, min(first + GROUP, tiers)):
                th = theta_v[jb, k]
                north = jnp.concatenate([th[1:], theta_v[jb + 1, k][:1]], axis=0)
                face = 0.5 * (th + north)
                volume = jnp.where(k < wet, dz[k] * dx, 0.0)
                moved = volume * speed_v[jb, k]
                heat = heat + moved * face
                warm = warm + volume * face
                water = water + volume
                place = jnp.clip(
                    (face - THERMAL_FLOOR) * (THERMAL_BINS / THERMAL_RANGE),
                    0.0, THERMAL_BINS - 1.0,
                )
                low = jnp.minimum(jnp.floor(place), THERMAL_BINS - 2.0)
                upper = moved * (place - low)
                under = moved - upper
                high = jnp.floor((low + 0.5) * (1.0 / DIGIT))
                digit = low - DIGIT * high
                pick = high * OCEAN_REGIONS + reg
                pick2 = jnp.concatenate([pick, pick - 1.0], axis=0).astype(BF)
                digit2 = jnp.concatenate([digit, digit], axis=0).astype(BF)
                under2, upper2 = two_parts(under), two_parts(upper)
                levels.append(two_parts(moved))
                lefts.append(
                    jnp.concatenate(
                        [
                            jnp.where(pick2 == jnp.asarray(2 * n, BF), one, zero)
                            for n in range(HIGHS * OCEAN_REGIONS // 2)
                        ],
                        axis=0,
                    )
                )
                hits = [digit2 == jnp.asarray(n, BF) for n in range(DIGIT)]
                tent = [jnp.where(hits[0], under2, zero)]
                for n in range(1, DIGIT):
                    tent.append(jnp.where(hits[n], under2, jnp.where(hits[n - 1], upper2, zero)))
                tent.append(jnp.where(hits[DIGIT - 1], upper2, zero))
                rights.append(jnp.concatenate(tent, axis=0))
            part = lax.dot_general(
                jnp.concatenate(lefts, axis=1), jnp.concatenate(rights, axis=1), NT,
                preferred_element_type=F32,
            )
            acc = part if acc is None else acc + part

        def collapse(full):
            rows, cols = full.shape
            same = (iota((ROWS, cols), 0) == iota((ROWS, cols), 1) % ROWS)
            full = jnp.where(
                same[None], full.reshape(rows // ROWS, ROWS, cols), 0.0
            ).reshape(rows, cols)
            spread = (iota((cols, 128), 0) // (2 * ROWS) == iota((cols, 128), 1))
            out = jnp.dot(
                two_parts(full), jnp.where(spread, 1.0, 0.0).astype(BF),
                preferred_element_type=F32,
            )
            return out[:rows] + out[rows:]

        sums = collapse(acc)
        for b in range(OCEAN_REGIONS):
            line = sums[b * ROWS : (b + 1) * ROWS]
            for h in range(1, HIGHS):
                at = (h * OCEAN_REGIONS + b) * ROWS
                line = line + pltpu.roll(sums[at : at + ROWS], h * DIGIT, 1)
            buf[jb, pl.ds(b * ROWS, ROWS), :] = line
        reg2 = jnp.concatenate([reg, reg - 1.0], axis=0).astype(BF)
        basin = jnp.concatenate(
            [
                jnp.where(reg2 == jnp.asarray(2 * n, BF), one, zero)
                for n in range(OCEAN_REGIONS // 2)
            ],
            axis=0,
        )
        kept = levels + [two_parts(heat), two_parts(warm), two_parts(water)]
        while len(kept) % 8:
            kept.append(zero)
        table = collapse(
            lax.dot_general(
                basin, jnp.concatenate(kept, axis=0), NT, preferred_element_type=F32
            )
        )
        line = table[:ROWS]
        for b in range(1, OCEAN_REGIONS):
            line = line + pltpu.roll(table[b * ROWS : (b + 1) * ROWS], b * STRIDE, 1)
        buf[jb, pl.ds(OCEAN_REGIONS * ROWS, ROWS), :] = line

    def northern_row():
        @pl.when(mylat < nlat - 1)
        def _():
            for k in range(tiers):
                theta_v[blocks, k, pl.ds(0, 1), :] = edge_in[pl.ds(k, 1), :]
            depth_v[blocks, pl.ds(0, 1), :] = edge_in[pl.ds(tiers, 1), :].astype(jnp.int32)

        @pl.when(mylat == nlat - 1)
        def _():
            found = jnp.zeros((3 * top.shape[0], width), F32)
            for step in range(nlon):
                if step:
                    to_lon(top, top_in, top_send, top_recv, step).wait()
                block = top_in[step - 1] if step else top[...]
                owner = lax.rem(mylon + nlon - step, nlon)
                here = iota((width, width), 0) + owner * width == seam[...]
                found = found + jnp.dot(
                    exact_parts(block), jnp.where(here, 1.0, 0.0).astype(BF),
                    preferred_element_type=F32,
                )
            n = top.shape[0]
            row = found[:n] + found[n : 2 * n] + found[2 * n :]
            top[...] = row
            for k in range(tiers):
                theta_v[blocks, k, pl.ds(0, 1), :] = top[pl.ds(k, 1), :]
            depth_v[blocks, pl.ds(0, 1), :] = top[pl.ds(tiers, 1), :].astype(jnp.int32)

    def flux_middle():
        for step in range(1, nlon):
            to_lon(fx, fx_in, fx_send, fx_recv, step).wait()
        mine = fx[...]
        whole = jnp.zeros_like(mine)
        for owner in range(nlon):
            piece = mine
            for step in range(1, nlon):
                came = lax.rem(mylon + nlon - step, nlon)
                piece = jnp.where(came == owner, fx_in[step - 1], piece)
            whole = whole + piece
        fx[...] = whole
        total[...] = jnp.broadcast_to(jnp.sum(whole, axis=1, keepdims=True), total.shape)
        for step in range(1, nlat):
            to_lat(step).start()

    def flux_end():
        for step in range(1, nlat):
            to_lat(step).wait()
        before = jnp.zeros(total.shape, F32)
        for step in range(1, nlat):
            before = before + jnp.where(mylat >= step, total_in[step - 1], 0.0)
        until = (iota((height, height), 0) <= iota((height, height), 1)).astype(F32)
        run = jnp.dot(
            fx[:, pl.ds(0, height)], until, precision=HIGHEST, preferred_element_type=F32
        )
        out = implied_scale * (before[:, :1] + run)
        raw[blocks, 0, :, pl.ds(0, height)] = out

    def iteration(it, carry):
        speed_copy(it).wait()

        @pl.when(it + 1 < last)
        def _():
            theta_copy(it + 1).wait()

        @pl.when(it == min(3, last))
        def _():
            flux_middle()

        @pl.when(it == last)
        def _():
            edge_copy.wait()
            northern_row()

        compute(it)
        for offset in range(1, nlon):
            share(offset, buf.at[it], got.at[offset - 1, it]).start()
        return carry

    lax.fori_loop(0, blocks, iteration, 0)
    flux_end()
    for offset in range(1, nlon):
        share(offset, buf, got.at[offset - 1]).wait()
    for jb in range(blocks):
        both = tree([buf[jb]] + [got[offset - 1, jb] for offset in range(1, nlon)])
        raw[jb] = both.reshape(OCEAN_REGIONS + 1, ROWS, 128)


def finish(width_total, raw, class_o, stream_o, heat_o, implied_o):
    blocks, height = raw.shape[0] - 1, stream_o.shape[2]
    tiers = stream_o.shape[1]
    unit_scale = math.sqrt(THERMAL_BINS / (width_total * tiers))
    for b in range(OCEAN_REGIONS):
        class_o[b] = unit_scale * raw[:blocks, b]
    implied_o[...] = raw[blocks, 0, :OCEAN_REGIONS, :height]
    table = raw[:blocks, OCEAN_REGIONS].reshape(height, 128)
    dst, src = iota((128, 128), 0), iota((128, 128), 1)
    chain = (src // STRIDE == dst // STRIDE) & (src <= dst) & (src % STRIDE < tiers)
    stream = unit_scale * lax.dot_general(
        chain.astype(F32), table, NT, precision=HIGHEST, preferred_element_type=F32
    )
    for b in range(OCEAN_REGIONS):
        stream_o[b] = stream[b * STRIDE : b * STRIDE + tiers]
    row, lane = iota((4 * ROWS, 128), 0), iota((4 * ROWS, 128), 1)
    kind, place, slot = row // ROWS, row % ROWS, lane % STRIDE
    own = place == lane // STRIDE
    choose = (
        ((kind == 0) & own & (slot == tiers))
        | ((kind == 1) & own & (slot < tiers))
        | ((kind == 2) & (slot == tiers + 1))
        | ((kind == 3) & (slot == tiers + 2))
    )
    rows = lax.dot_general(
        choose.astype(F32), table, NT, precision=HIGHEST, preferred_element_type=F32
    )
    mean = rows[2 * ROWS : 3 * ROWS] / rows[3 * ROWS :]
    heat = (unit_scale / 16.0) * (rows[:ROWS] - rows[ROWS : 2 * ROWS] * mean)
    heat_o[...] = heat[:OCEAN_REGIONS]


def body(speed, theta, dz, dx, area, flux, depth, region, seam):
    tiers, height, width = theta.shape
    nlon, nlat = lax.axis_size("lon"), lax.axis_size("lat")
    blocks = height // ROWS
    edge_rows = -(-(tiers + 1) // 8) * 8
    pad = -(-height // 128) * 128
    flat = (blocks, ROWS, width)
    any_spec = pl.BlockSpec(memory_space=pltpu.HBM)
    vmem = pl.BlockSpec(memory_space=pltpu.VMEM)
    dma = pltpu.SemaphoreType.DMA
    raw = pl.pallas_call(
        functools.partial(kernel, nlon, nlat, width * nlon, height * nlat),
        name="transport",
        out_shape=jax.ShapeDtypeStruct((blocks + 1, OCEAN_REGIONS + 1, ROWS, pad), F32),
        in_specs=[pl.BlockSpec(memory_space=pltpu.SMEM)] + [any_spec] * 7 + [vmem],
        out_specs=vmem,
        scratch_shapes=[
            pltpu.VMEM((blocks, tiers, ROWS, width), F32),
            pltpu.VMEM((blocks + 1, tiers, ROWS, width), F32),
            pltpu.VMEM(flat, F32),
            pltpu.VMEM(flat, F32),
            pltpu.VMEM(flat, F32),
            pltpu.VMEM((blocks + 1, ROWS, width), jnp.int32),
            pltpu.VMEM(flat, jnp.int32),
            pltpu.VMEM((edge_rows, width), F32),
            pltpu.VMEM((edge_rows, width), F32),
            pltpu.VMEM((edge_rows, width), F32),
            pltpu.VMEM((nlon - 1, edge_rows, width), F32),
            pltpu.VMEM((ROWS, pad), F32),
            pltpu.VMEM((nlon - 1, ROWS, pad), F32),
            pltpu.VMEM((ROWS, 128), F32),
            pltpu.VMEM((nlat - 1, ROWS, 128), F32),
            pltpu.VMEM((blocks, 5 * ROWS, 128), F32),
            pltpu.VMEM((nlon - 1, blocks, 5 * ROWS, 128), F32),
            dma((2, blocks)),
            dma((5,)),
            dma((2,)),
            dma((nlon - 1,)),
            dma((nlon - 1,)),
            dma((nlon - 1,)),
            dma((nlon - 1,)),
            dma((nlat - 1,)),
            dma((nlat - 1,)),
            dma((nlon - 1,)),
            dma((nlon - 1,)),
        ],
        compiler_params=pltpu.CompilerParams(
            collective_id=0, has_side_effects=True, vmem_limit_bytes=67043328 - (blocks + 1) * (OCEAN_REGIONS + 1) * ROWS * pad * 4 - 8192
        ),
    )(
        dz,
        speed.reshape(tiers, *flat),
        theta.reshape(tiers, *flat),
        dx.reshape(flat),
        area.reshape(flat),
        flux.reshape(flat),
        depth.reshape(flat),
        region.reshape(flat),
        seam.reshape(1, width),
    )
    out = pl.pallas_call(
        functools.partial(finish, width * nlon),
        name="finish",
        out_shape=(
            jax.ShapeDtypeStruct((OCEAN_REGIONS, blocks, ROWS, THERMAL_BINS), F32),
            jax.ShapeDtypeStruct((OCEAN_REGIONS, tiers, height), F32),
            jax.ShapeDtypeStruct((OCEAN_REGIONS, height), F32),
            jax.ShapeDtypeStruct((OCEAN_REGIONS, height), F32),
        ),
        in_specs=[vmem],
        out_specs=(vmem,) * 4,
        compiler_params=pltpu.CompilerParams(vmem_limit_bytes=8 << 20),
    )(raw)
    classes = out[0].reshape(OCEAN_REGIONS, height, THERMAL_BINS)
    return (classes, jnp.swapaxes(out[1], 1, 2), out[2], out[3])


def solution(mesh):
    in_specs = (
        P(None, "lat", "lon"),
        P(None, "lat", "lon"),
        P(),
        P("lat", "lon"),
        P("lat", "lon"),
        P("lat", "lon"),
        P("lat", "lon"),
        P("lat", "lon"),
        P("lon"),
    )
    out_specs = (P(None, "lat", None), P(None, "lat", None), P(None, "lat"), P(None, "lat"))
    return jax.shard_map(body, mesh=mesh, in_specs=in_specs, out_specs=out_specs, check_vma=False)
```

profile of v0, /device:TPU:0, one launch (start us, length us, event | category | flops | bytes accessed | tf_op | source)
XLA Modules:
  0.0 25.4 jit_solution(12979069593004871916)
XLA Ops:
  0.6 22.9 %transport.1.raw = f32[9,5,8,128]{3,2,1,0:T(8,128)} custom-call(f32[16]{0:T(128)} %dz.1, f32[16,8,8,256]{3,2,1,0:T(8,128)} %bitcast.10, f32[16,8,8,256]{3,2,1,0:T(8,128)} %bitcast.11, f32[8,8,256]{2,1,0:T(8,128)} %bitcast.12, f32[8,8,256]{2,1,0:T(8,128)} %bitcast.13, f32[8,8,256]{2,1,0:T(8,128)} %bitcast.14, s32[8,8,256]{2,1,0:T(8,128)} %bitcast.15, ...), custom_call_target="tpu_custom_call" | custom-call | tf_op jit(solution)/shard_map/transport/pallas_call | solution.py:395
  23.6 0.0 copy-start
  23.6 0.9 %copy-done = f32[9,5,8,128]{3,2,1,0:T(8,128)S(1)} copy-done((f32[9,5,8,128]{3,2,1,0:T(8,128)S(1)}, f32[9,5,8,128]{3,2,1,0:T(8,128)}, u32[]{:S(2)}) %copy-start) | copy-done | bytes 184344
  24.5 0.9 %finish.1 = (f32[4,8,8,128]{3,2,1,0:T(8,128)}, f32[4,16,64]{2,1,0:T(8,128)}, f32[4,64]{1,0:T(4,128)}, f32[4,64]{1,0:T(4,128)}) custom-call(f32[9,5,8,128]{3,2,1,0:T(8,128)S(1)} %copy-done), custom_call_target="tpu_custom_call" | custom-call | tf_op jit(solution)/shard_map/finish/pallas_call | solution.py:445
Async XLA Ops:
  23.6 0.9 %copy-start = (f32[9,5,8,128]{3,2,1,0:T(8,128)S(1)}, f32[9,5,8,128]{3,2,1,0:T(8,128)}, u32[]{:S(2)}) copy-start(f32[9,5,8,128]{3,2,1,0:T(8,128)} %transport.1.raw) | copy-start | bytes 552964
where the time goes:
time: 25.6 us; the launch traced here: 25.4 us
  Pallas kernels  23.8 us (93%)
  local copies, waits for them, and re-layouts  0.92 us (4%)
  between operations  0.65 us (3%)
    pallas_call x1, Pallas kernels, body(): pl.pallas_call(functools.partial(kernel, nlon, nlat, width * nlon, height...  22.9 us
    unnamed x2, local copies, waits for them, and re-layouts  0.92 us
    pallas_call x1, Pallas kernels, body(): pl.pallas_call(functools.partial(finish, width * nlon), name='finish', ou...  0.86 us

commit v1 on v0

v1 whole, which is shorter than its diff:
```python
import functools
import math

import jax
import jax.numpy as jnp
from jax import lax
from jax.experimental import pallas as pl
from jax.experimental.pallas import tpu as pltpu
from jax.sharding import PartitionSpec as P

THERMAL_BINS = 128
OCEAN_REGIONS = 4
THERMAL_FLOOR = -2.0
THERMAL_RANGE = 32.0

ROWS = 8
DIGIT = 16
HIGHS = THERMAL_BINS // DIGIT
PAIRS = OCEAN_REGIONS // 2
GROUP = 4
STRIDE = 32
MESH = pl.DeviceIdType.MESH
NT = (((1,), (1,)), ((), ()))
HIGHEST = lax.Precision.HIGHEST
BF = jnp.bfloat16
F32 = jnp.float32


def iota(shape, dim):
    return lax.broadcasted_iota(jnp.int32, shape, dim)


def two_parts(x):
    high = x.astype(BF).astype(F32)
    return jnp.concatenate([high, x - high], axis=0).astype(BF)


def exact_parts(x):
    high = x.astype(BF).astype(F32)
    rest = x - high
    mid = rest.astype(BF).astype(F32)
    return jnp.concatenate([high.astype(BF), mid.astype(BF), (rest - mid).astype(BF)], axis=0)


def kernel(
    nlon, nlat, width_total, height_total,
    dz, speed, theta, dx_all, area, flux, depth, region, seam,
    raw,
    edge, edge_in, top, top_in, cap, fx, fx_in, total, total_in, buf, got,
    edge_sem, top_send, top_recv, fx_send, fx_recv, tot_send, tot_recv,
    sum_send, sum_recv,
):
    tiers, blocks, _, width = theta.shape
    height = blocks * ROWS
    mylon, mylat = lax.axis_index("lon"), lax.axis_index("lat")
    implied_scale = 2.0 / math.sqrt(width_total * height_total)
    last = blocks - 1

    barrier = pltpu.get_barrier_semaphore()
    for step in range(1, nlon):
        peer = lax.rem(mylon + step, nlon)
        pl.semaphore_signal(barrier, inc=1, device_id=(peer, mylat), device_id_type=MESH)
    for step in range(1, nlat):
        peer = lax.rem(mylat + step, nlat)
        pl.semaphore_signal(barrier, inc=1, device_id=(mylon, peer), device_id_type=MESH)

    def flux_start():
        region_all = region[...].reshape(height, width)
        product = flux[...].reshape(height, width) * area[...].reshape(height, width)
        fx_rows = jnp.zeros((ROWS, height), F32)
        for b in range(OCEAN_REGIONS):
            part = lax.dot_general(
                jnp.ones((ROWS, width), F32),
                jnp.where(region_all == b, product, 0.0),
                NT, precision=HIGHEST, preferred_element_type=F32,
            )
            fx_rows = jnp.where(iota((ROWS, height), 0) == b, part, fx_rows)
        fx[...] = jnp.zeros_like(fx)
        fx[:, pl.ds(0, height)] = fx_rows

    edge[...] = jnp.zeros_like(edge)
    top[...] = jnp.zeros_like(top)
    for k in range(tiers):
        edge[pl.ds(k, 1), :] = theta[k, 0, pl.ds(0, 1), :]
        top[pl.ds(k, 1), :] = theta[k, last, pl.ds(ROWS - 1, 1), :]
    edge[pl.ds(tiers, 1), :] = depth[0, pl.ds(0, 1), :].astype(F32)
    top[pl.ds(tiers, 1), :] = depth[last, pl.ds(ROWS - 1, 1), :].astype(F32)
    flux_start()

    edge_copy = pltpu.make_async_remote_copy(
        edge, edge_in, edge_sem.at[0], edge_sem.at[1],
        device_id=(mylon, lax.rem(mylat + nlat - 1, nlat)), device_id_type=MESH,
    )

    def to_lon(src, dst, send, recv, step):
        return pltpu.make_async_remote_copy(
            src, dst.at[step - 1], send.at[step - 1], recv.at[step - 1],
            device_id=(lax.rem(mylon + step, nlon), mylat), device_id_type=MESH,
        )

    def to_lat(step):
        return pltpu.make_async_remote_copy(
            total, total_in.at[step - 1], tot_send.at[step - 1], tot_recv.at[step - 1],
            device_id=(mylon, lax.rem(mylat + step, nlat)), device_id_type=MESH,
        )

    def across(offset):
        peer = mylon
        for bit in range(nlon.bit_length() - 1):
            stride = 1 << bit
            if offset & stride:
                peer = peer + stride * (1 - 2 * lax.rem(lax.div(mylon, stride), 2))
        return peer

    def share(offset, src, dst):
        return pltpu.make_async_remote_copy(
            src, dst, sum_send.at[offset - 1], sum_recv.at[offset - 1],
            device_id=(across(offset), mylat), device_id_type=MESH,
        )

    def tree(parts):
        while len(parts) > 1:
            parts = [parts[n] + parts[n + 1] for n in range(0, len(parts), 2)]
        return parts[0]

    def first_sends():
        pl.semaphore_wait(barrier, nlon - 1 + nlat - 1)
        edge_copy.start()
        for step in range(1, nlon):
            to_lon(fx, fx_in, fx_send, fx_recv, step).start()

        @pl.when(mylat == nlat - 1)
        def _():
            for step in range(1, nlon):
                to_lon(top, top_in, top_send, top_recv, step).start()

    def compute(jb, cap_row):
        reg = region[jb].astype(F32)
        dx = dx_all[jb]
        deep = depth[jb].astype(F32)

        def above(own, k):
            row = theta[k, jb + 1, pl.ds(0, 1), :] if cap_row is None else cap_row(k)
            return jnp.concatenate([own[1:], row], axis=0)

        def twice(x, y):
            return jnp.concatenate([x, y], axis=0).astype(BF)

        depth_row = (
            depth[jb + 1, pl.ds(0, 1), :].astype(F32) if cap_row is None else cap_row(tiers)
        )
        wet = jnp.minimum(deep, jnp.concatenate([deep[1:], depth_row], axis=0))
        one, zero = jnp.ones((2 * ROWS, width), BF), jnp.zeros((2 * ROWS, width), BF)
        reg2 = twice(reg, reg - 1.0)
        here = [
            jnp.where(reg2 == jnp.asarray(2 * n, BF), one, zero) for n in range(PAIRS)
        ]
        heat = jnp.zeros((ROWS, width), F32)
        warm = jnp.zeros((ROWS, width), F32)
        water = jnp.zeros((ROWS, width), F32)
        kept = []
        acc = None
        for first in range(0, tiers, GROUP):
            tents, picks = [], []
            for k in range(first, min(first + GROUP, tiers)):
                th = theta[k, jb]
                both = th + above(th, k)
                face = 0.5 * both
                volume = jnp.where(wet > float(k), dz[k] * dx, 0.0)
                moved = volume * speed[k, jb]
                heat = heat + moved * face
                warm = warm + volume * face
                water = water + volume
                place = jnp.clip(
                    (face - THERMAL_FLOOR) * (THERMAL_BINS / THERMAL_RANGE),
                    0.0, THERMAL_BINS - 1.0,
                )
                low = jnp.minimum(jnp.floor(place), THERMAL_BINS - 2.0)
                upper = moved * (place - low)
                under = moved - upper
                high = jnp.floor(low * (1.0 / DIGIT))
                digit = low - DIGIT * high
                high2 = twice(high, high)
                digit2 = twice(digit, digit - 8.0)
                under_h = under.astype(BF).astype(F32)
                upper_h = upper.astype(BF).astype(F32)
                under_l, upper_l = under - under_h, upper - upper_h
                hits = [digit2 == jnp.asarray(n, BF) for n in range(-1, 8)]
                tent = []
                for low_half, high_half in ((under_h, upper_h), (under_l, upper_l)):
                    low2, up2 = twice(low_half, low_half), twice(high_half, high_half)
                    for n in range(8):
                        tent.append(
                            jnp.where(hits[n + 1], low2, jnp.where(hits[n], up2, zero))
                        )
                ending = twice(digit, digit) == jnp.asarray(DIGIT - 1, BF)
                tent.append(jnp.where(ending, twice(upper_h, upper_l), zero))
                tents.append(jnp.concatenate(tent, axis=0))
                kept.append(two_parts(moved))
                chosen = [high2 == jnp.asarray(n, BF) for n in range(HIGHS)]
                picks.append(
                    jnp.concatenate(
                        [
                            jnp.where(chosen[n], here[pair], zero)
                            for pair in range(PAIRS)
                            for n in range(HIGHS)
                        ],
                        axis=0,
                    )
                )
            part = lax.dot_general(
                jnp.concatenate(tents, axis=1), jnp.concatenate(picks, axis=1), NT,
                preferred_element_type=F32,
            )
            acc = part if acc is None else acc + part

        lane = iota((ROWS, 128), 1)
        row = iota((ROWS, 128), 0)

        def align(x, slot):
            source = (lane + row + (128 - slot)) % 128
            return jnp.take_along_axis(x, source, axis=1, mode="promise_in_bounds")

        for pair in range(PAIRS):
            cols = acc[:, 128 * pair : 128 * pair + 128]
            held = []
            for half in range(2):
                out = jnp.zeros((ROWS, 128), F32)
                for n in range(8):
                    at = 16 * n + 8 * half
                    one_tent = cols[at : at + ROWS] + cols[128 + at : 128 + at + ROWS]
                    out = jnp.where(lane % 8 == n, align(one_tent, n), out)
                held.append(out)
            final = cols[256 : 256 + ROWS] + cols[256 + ROWS :]
            held[0] = held[0] + jnp.where(lane % 8 == 0, align(final, DIGIT), 0.0)
            left = lane % 16 < 8
            buf[jb, pl.ds(2 * pair * ROWS, ROWS), :] = jnp.where(
                left, held[0], pltpu.roll(held[1], 8, 1)
            )
            buf[jb, pl.ds((2 * pair + 1) * ROWS, ROWS), :] = jnp.where(
                left, pltpu.roll(held[0], 120, 1), held[1]
            )
        kept = kept + [two_parts(heat), two_parts(warm), two_parts(water)]
        nothing = jnp.zeros((ROWS, width), F32)
        basin = []
        for b in range(OCEAN_REGIONS):
            basin += [twice(jnp.where(reg == float(b), 1.0, 0.0), nothing), zero]
        table = lax.dot_general(
            jnp.concatenate(kept, axis=0), jnp.concatenate(basin, axis=0), NT,
            preferred_element_type=F32,
        )
        line = jnp.zeros((ROWS, 128), F32)
        for k in range(len(kept)):
            at = 2 * ROWS * k
            whole = table[at : at + ROWS] + table[at + ROWS : at + 2 * ROWS]
            line = jnp.where(lane % STRIDE == k, align(whole, k), line)
        buf[jb, pl.ds(OCEAN_REGIONS * ROWS, ROWS), :] = line
        for offset in range(1, nlon):
            share(offset, buf.at[jb], got.at[offset - 1, jb]).start()

    def northern_row():
        edge_copy.wait()

        @pl.when(mylat < nlat - 1)
        def _():
            cap[...] = edge_in[...]

        @pl.when(mylat == nlat - 1)
        def _():
            found = jnp.zeros((3 * top.shape[0], width), F32)
            for step in range(nlon):
                if step:
                    to_lon(top, top_in, top_send, top_recv, step).wait()
                block = top_in[step - 1] if step else top[...]
                owner = lax.rem(mylon + nlon - step, nlon)
                here = iota((width, width), 0) + owner * width == seam[...]
                found = found + jnp.dot(
                    exact_parts(block), jnp.where(here, 1.0, 0.0).astype(BF),
                    preferred_element_type=F32,
                )
            n = top.shape[0]
            cap[...] = found[:n] + found[n : 2 * n] + found[2 * n :]

    def flux_middle():
        for step in range(1, nlon):
            to_lon(fx, fx_in, fx_send, fx_recv, step).wait()
        mine = fx[...]
        whole = jnp.zeros_like(mine)
        for owner in range(nlon):
            piece = mine
            for step in range(1, nlon):
                came = lax.rem(mylon + nlon - step, nlon)
                piece = jnp.where(came == owner, fx_in[step - 1], piece)
            whole = whole + piece
        fx[...] = whole
        total[...] = jnp.broadcast_to(jnp.sum(whole, axis=1, keepdims=True), total.shape)
        for step in range(1, nlat):
            to_lat(step).start()

    def flux_end():
        for step in range(1, nlat):
            to_lat(step).wait()
        before = jnp.zeros(total.shape, F32)
        for step in range(1, nlat):
            before = before + jnp.where(mylat >= step, total_in[step - 1], 0.0)
        until = (iota((height, height), 0) <= iota((height, height), 1)).astype(F32)
        run = jnp.dot(
            fx[:, pl.ds(0, height)], until, precision=HIGHEST, preferred_element_type=F32
        )
        out = implied_scale * (before[:, :1] + run)
        raw[blocks, 0, :, pl.ds(0, height)] = out

    def iteration(it, carry):
        @pl.when(it == min(4, last - 1))
        def _():
            flux_middle()

        compute(it, None)
        return carry

    first_sends()
    lax.fori_loop(0, last, iteration, 0)
    northern_row()
    compute(last, lambda k: cap[pl.ds(k, 1), :])
    flux_end()
    for offset in range(1, nlon):
        share(offset, buf, got.at[offset - 1]).wait()
    for jb in range(blocks):
        both = tree([buf[jb]] + [got[offset - 1, jb] for offset in range(1, nlon)])
        raw[jb] = both.reshape(OCEAN_REGIONS + 1, ROWS, 128)


def finish(width_total, raw, class_o, stream_o, heat_o, implied_o):
    blocks, height = raw.shape[0] - 1, stream_o.shape[2]
    tiers = stream_o.shape[1]
    unit_scale = math.sqrt(THERMAL_BINS / (width_total * tiers))
    for b in range(OCEAN_REGIONS):
        class_o[b] = unit_scale * raw[:blocks, b]
    implied_o[...] = raw[blocks, 0, :OCEAN_REGIONS, :height]
    table = raw[:blocks, OCEAN_REGIONS].reshape(height, 128)
    dst, src = iota((128, 128), 0), iota((128, 128), 1)
    chain = (src // STRIDE == dst // STRIDE) & (src <= dst) & (src % STRIDE < tiers)
    stream = unit_scale * lax.dot_general(
        chain.astype(F32), table, NT, precision=HIGHEST, preferred_element_type=F32
    )
    for b in range(OCEAN_REGIONS):
        stream_o[b] = stream[b * STRIDE : b * STRIDE + tiers]
    row, lane = iota((4 * ROWS, 128), 0), iota((4 * ROWS, 128), 1)
    kind, place, slot = row // ROWS, row % ROWS, lane % STRIDE
    own = place == lane // STRIDE
    choose = (
        ((kind == 0) & own & (slot == tiers))
        | ((kind == 1) & own & (slot < tiers))
        | ((kind == 2) & (slot == tiers + 1))
        | ((kind == 3) & (slot == tiers + 2))
    )
    rows = lax.dot_general(
        choose.astype(F32), table, NT, precision=HIGHEST, preferred_element_type=F32
    )
    mean = rows[2 * ROWS : 3 * ROWS] / rows[3 * ROWS :]
    heat = (unit_scale / 16.0) * (rows[:ROWS] - rows[ROWS : 2 * ROWS] * mean)
    heat_o[...] = heat[:OCEAN_REGIONS]


def body(speed, theta, dz, dx, area, flux, depth, region, seam):
    tiers, height, width = theta.shape
    nlon, nlat = lax.axis_size("lon"), lax.axis_size("lat")
    blocks = height // ROWS
    edge_rows = -(-(tiers + 1) // 8) * 8
    pad = -(-height // 128) * 128
    flat = (blocks, ROWS, width)
    vmem = pl.BlockSpec(memory_space=pltpu.VMEM)
    dma = pltpu.SemaphoreType.DMA
    raw = pl.pallas_call(
        functools.partial(kernel, nlon, nlat, width * nlon, height * nlat),
        name="transport",
        out_shape=jax.ShapeDtypeStruct((blocks + 1, OCEAN_REGIONS + 1, ROWS, pad), F32),
        in_specs=[pl.BlockSpec(memory_space=pltpu.SMEM)] + [vmem] * 8,
        out_specs=vmem,
        scratch_shapes=[
            pltpu.VMEM((edge_rows, width), F32),
            pltpu.VMEM((edge_rows, width), F32),
            pltpu.VMEM((edge_rows, width), F32),
            pltpu.VMEM((nlon - 1, edge_rows, width), F32),
            pltpu.VMEM((edge_rows, width), F32),
            pltpu.VMEM((ROWS, pad), F32),
            pltpu.VMEM((nlon - 1, ROWS, pad), F32),
            pltpu.VMEM((ROWS, 128), F32),
            pltpu.VMEM((nlat - 1, ROWS, 128), F32),
            pltpu.VMEM((blocks, 5 * ROWS, 128), F32),
            pltpu.VMEM((nlon - 1, blocks, 5 * ROWS, 128), F32),
            dma((2,)),
            dma((nlon - 1,)),
            dma((nlon - 1,)),
            dma((nlon - 1,)),
            dma((nlon - 1,)),
            dma((nlat - 1,)),
            dma((nlat - 1,)),
            dma((nlon - 1,)),
            dma((nlon - 1,)),
        ],
        compiler_params=pltpu.CompilerParams(
            collective_id=0, has_side_effects=True, vmem_limit_bytes=40 << 20
        ),
    )(
        dz,
        speed.reshape(tiers, *flat),
        theta.reshape(tiers, *flat),
        dx.reshape(flat),
        area.reshape(flat),
        flux.reshape(flat),
        depth.reshape(flat),
        region.reshape(flat),
        seam.reshape(1, width),
    )
    out = pl.pallas_call(
        functools.partial(finish, width * nlon),
        name="finish",
        out_shape=(
            jax.ShapeDtypeStruct((OCEAN_REGIONS, blocks, ROWS, THERMAL_BINS), F32),
            jax.ShapeDtypeStruct((OCEAN_REGIONS, tiers, height), F32),
            jax.ShapeDtypeStruct((OCEAN_REGIONS, height), F32),
            jax.ShapeDtypeStruct((OCEAN_REGIONS, height), F32),
        ),
        in_specs=[vmem],
        out_specs=(vmem,) * 4,
        compiler_params=pltpu.CompilerParams(vmem_limit_bytes=8 << 20),
    )(raw)
    classes = out[0].reshape(OCEAN_REGIONS, height, THERMAL_BINS)
    return (classes, jnp.swapaxes(out[1], 1, 2), out[2], out[3])


def solution(mesh):
    in_specs = (
        P(None, "lat", "lon"),
        P(None, "lat", "lon"),
        P(),
        P("lat", "lon"),
        P("lat", "lon"),
        P("lat", "lon"),
        P("lat", "lon"),
        P("lat", "lon"),
        P("lon"),
    )
    out_specs = (P(None, "lat", None), P(None, "lat", None), P(None, "lat"), P(None, "lat"))
    return jax.shard_map(body, mesh=mesh, in_specs=in_specs, out_specs=out_specs, check_vma=False)
```

time: 25.6 us -> 27.9 us (1.090)
  local copies, waits for them, and re-layouts: 0.92 us -> 7.31 us
  Pallas kernels: 23.8 us -> 19.5 us
    unnamed x2 -> x18, local copies, waits for them, and re-layouts: 0.92 us -> 7.31 us
    pallas_call x1, Pallas kernels: 22.9 us -> 18.6 us  [body(): pl.pallas_call(functools.partial(kernel, nlon, nlat, width * nlon, height...]
where the time goes in v1:
time: 27.9 us; the launch traced here: 27.5 us
  Pallas kernels  19.5 us (70%)
  local copies, waits for them, and re-layouts  7.31 us (26%)
  between operations  0.67 us (2%)
    pallas_call x1, Pallas kernels, body(): pl.pallas_call(functools.partial(kernel, nlon, nlat, width * nlon, height...  18.6 us
    unnamed x18, local copies, waits for them, and re-layouts  7.31 us
    pallas_call x1, Pallas kernels, body(): pl.pallas_call(functools.partial(finish, width * nlon), name='finish', ou...  0.86 us

profile of v1, /device:TPU:0, one launch (start us, length us, event | category | flops | bytes accessed | tf_op | source)
XLA Modules:
  0.0 27.5 jit_solution(14542575822810153625)
XLA Ops:
  0.6 0.0 copy-start.7
  0.6 0.0 copy-start.8
  0.7 0.7 %copy-done.7 = s32[256]{0:T(256)S(1)} copy-done((s32[256]{0:T(256)S(1)}, s32[256]{0:T(256)}, u32[]{:S(2)}) %copy-start.7) | copy-done | bytes 1048
  1.3 0.0 copy-done.8
  1.3 0.0 copy-start
  1.3 1.2 %copy-done = f32[16,64,256]{2,1,0:T(8,128)S(1)} copy-done((f32[16,64,256]{2,1,0:T(8,128)S(1)}, f32[16,64,256]{2,1,0:T(8,128)}, u32[]{:S(2)}) %copy-start) | copy-done | bytes 1048600
  2.5 0.0 copy-start.1
  2.5 1.2 %copy-done.1 = f32[16,64,256]{2,1,0:T(8,128)S(1)} copy-done((f32[16,64,256]{2,1,0:T(8,128)S(1)}, f32[16,64,256]{2,1,0:T(8,128)}, u32[]{:S(2)}) %copy-start.1) | copy-done | bytes 1048600
  3.8 0.0 copy-start.2
  3.8 0.8 %copy-done.2 = f32[64,256]{1,0:T(8,128)S(1)} copy-done((f32[64,256]{1,0:T(8,128)S(1)}, f32[64,256]{1,0:T(8,128)}, u32[]{:S(2)}) %copy-start.2) | copy-done | bytes 65560
  4.6 0.0 copy-start.3
  4.6 0.8 %copy-done.3 = f32[64,256]{1,0:T(8,128)S(1)} copy-done((f32[64,256]{1,0:T(8,128)S(1)}, f32[64,256]{1,0:T(8,128)}, u32[]{:S(2)}) %copy-start.3) | copy-done | bytes 65560
  5.4 0.0 copy-start.4
  5.5 0.8 %copy-done.4 = f32[64,256]{1,0:T(8,128)S(1)} copy-done((f32[64,256]{1,0:T(8,128)S(1)}, f32[64,256]{1,0:T(8,128)}, u32[]{:S(2)}) %copy-start.4) | copy-done | bytes 65560
  6.3 0.0 copy-start.5
  6.3 0.8 %copy-done.5 = s32[64,256]{1,0:T(8,128)S(1)} copy-done((s32[64,256]{1,0:T(8,128)S(1)}, s32[64,256]{1,0:T(8,128)}, u32[]{:S(2)}) %copy-start.5) | copy-done | bytes 65560
  7.1 0.0 copy-start.6
  7.1 0.8 %copy-done.6 = s32[64,256]{1,0:T(8,128)S(1)} copy-done((s32[64,256]{1,0:T(8,128)S(1)}, s32[64,256]{1,0:T(8,128)}, u32[]{:S(2)}) %copy-start.6) | copy-done | bytes 65560
  8.0 18.6 %transport.1.raw = f32[9,5,8,128]{3,2,1,0:T(8,128)S(1)} custom-call(f32[16]{0:T(128)S(1)} %copy-done.8, f32[16,8,8,256]{3,2,1,0:T(8,128)S(1)} %bitcast.10, f32[16,8,8,256]{3,2,1,0:T(8,128)S(1)} %bitcast.11, f32[8,8,256]{2,1,0:T(8,128)S(1)} %bitcast.12, f32[8,8,256]{2,1,0:T(8,128)S(1)} %bitcast.13, f32[8,8,256]{2,1,0:T(8,128)S(1)} %bitcast.14, ...), custom_call_target="tpu_custom_call" | custom-call | tf_op jit(solution)/shard_map/transport/pallas_call | solution.py:374
  26.6 0.9 %finish.1 = (f32[4,8,8,128]{3,2,1,0:T(8,128)}, f32[4,16,64]{2,1,0:T(8,128)}, f32[4,64]{1,0:T(4,128)}, f32[4,64]{1,0:T(4,128)}) custom-call(f32[9,5,8,128]{3,2,1,0:T(8,128)S(1)} %transport.1.raw), custom_call_target="tpu_custom_call" | custom-call | tf_op jit(solution)/shard_map/finish/pallas_call | solution.py:416
Async XLA Ops:
  0.6 0.7 %copy-start.7 = (s32[256]{0:T(256)S(1)}, s32[256]{0:T(256)}, u32[]{:S(2)}) copy-start(s32[256]{0:T(256)} %param.17) | copy-start | bytes 3076
  0.6 0.7 %copy-start.8 = (f32[16]{0:T(128)S(1)}, f32[16]{0:T(128)}, u32[]{:S(2)}) copy-start(f32[16]{0:T(128)} %dz.1) | copy-start | bytes 196
  1.3 1.2 %copy-start = (f32[16,64,256]{2,1,0:T(8,128)S(1)}, f32[16,64,256]{2,1,0:T(8,128)}, u32[]{:S(2)}) copy-start(f32[16,64,256]{2,1,0:T(8,128)} %param.9) | copy-start | bytes 3145732
  2.5 1.2 %copy-start.1 = (f32[16,64,256]{2,1,0:T(8,128)S(1)}, f32[16,64,256]{2,1,0:T(8,128)}, u32[]{:S(2)}) copy-start(f32[16,64,256]{2,1,0:T(8,128)} %param.10) | copy-start | bytes 3145732
  3.8 0.8 %copy-start.2 = (f32[64,256]{1,0:T(8,128)S(1)}, f32[64,256]{1,0:T(8,128)}, u32[]{:S(2)}) copy-start(f32[64,256]{1,0:T(8,128)} %param.12) | copy-start | bytes 196612
  4.6 0.8 %copy-start.3 = (f32[64,256]{1,0:T(8,128)S(1)}, f32[64,256]{1,0:T(8,128)}, u32[]{:S(2)}) copy-start(f32[64,256]{1,0:T(8,128)} %param.13) | copy-start | bytes 196612
  5.4 0.8 %copy-start.4 = (f32[64,256]{1,0:T(8,128)S(1)}, f32[64,256]{1,0:T(8,128)}, u32[]{:S(2)}) copy-start(f32[64,256]{1,0:T(8,128)} %param.14) | copy-start | bytes 196612
  6.3 0.8 %copy-start.5 = (s32[64,256]{1,0:T(8,128)S(1)}, s32[64,256]{1,0:T(8,128)}, u32[]{:S(2)}) copy-start(s32[64,256]{1,0:T(8,128)} %param.15) | copy-start | bytes 196612
  7.1 0.8 %copy-start.6 = (s32[64,256]{1,0:T(8,128)S(1)}, s32[64,256]{1,0:T(8,128)}, u32[]{:S(2)}) copy-start(s32[64,256]{1,0:T(8,128)} %param.16) | copy-start | bytes 196612

commit v2 on v1

--- a/solution.py
+++ b/solution.py
@@ -19,6 +19,7 @@
 PAIRS = OCEAN_REGIONS // 2
 GROUP = 4
 STRIDE = 32
+CUTS = (2, 4, 6)
 MESH = pl.DeviceIdType.MESH
 NT = (((1,), (1,)), ((), ()))
 HIGHEST = lax.Precision.HIGHEST
@@ -43,17 +44,16 @@
 
 
 def kernel(
-    nlon, nlat, width_total, height_total,
+    nlon, nlat,
+    dz_h, speed_h, theta_h, dx_h, area_h, flux_h, depth_h, region_h, seam_h,
+    raw,
     dz, speed, theta, dx_all, area, flux, depth, region, seam,
-    raw,
-    edge, edge_in, top, top_in, cap, fx, fx_in, total, total_in, buf, got,
-    edge_sem, top_send, top_recv, fx_send, fx_recv, tot_send, tot_recv,
+    edge, edge_in, top, top_in, cap, total, total_in, buf, got,
+    big_sem, small_sem, edge_sem, top_send, top_recv, tot_send, tot_recv,
     sum_send, sum_recv,
 ):
-    tiers, blocks, _, width = theta.shape
-    height = blocks * ROWS
+    tiers, blocks, _, width = theta_h.shape
     mylon, mylat = lax.axis_index("lon"), lax.axis_index("lat")
-    implied_scale = 2.0 / math.sqrt(width_total * height_total)
     last = blocks - 1
 
     barrier = pltpu.get_barrier_semaphore()
@@ -64,28 +64,62 @@
         peer = lax.rem(mylat + step, nlat)
         pl.semaphore_signal(barrier, inc=1, device_id=(mylon, peer), device_id_type=MESH)
 
-    def flux_start():
-        region_all = region[...].reshape(height, width)
-        product = flux[...].reshape(height, width) * area[...].reshape(height, width)
-        fx_rows = jnp.zeros((ROWS, height), F32)
+    small = [
+        pltpu.make_async_copy(src, dst, small_sem.at[n])
+        for n, (src, dst) in enumerate(
+            [
+                (area_h, area),
+                (flux_h, flux),
+                (region_h, region),
+                (depth_h, depth),
+                (dx_h, dx_all),
+                (dz_h, dz),
+                (seam_h, seam),
+            ]
+        )
+    ]
+
+    def theta_copy(b):
+        return pltpu.make_async_copy(theta_h.at[:, b], theta.at[b], big_sem.at[0, b])
+
+    def speed_copy(b):
+        return pltpu.make_async_copy(speed_h.at[:, b], speed.at[b], big_sem.at[1, b])
+
+    for copy in small:
+        copy.start()
+    theta_copy(0).start()
+    theta_copy(last).start()
+    for b in range(blocks):
+        speed_copy(b).start()
+        if b + 1 < last:
+            theta_copy(b + 1).start()
+    for copy in small:
+        copy.wait()
+
+    def flux_total():
+        sums = [jnp.zeros((ROWS, width), F32)] * OCEAN_REGIONS
+        for jb in range(blocks):
+            product = flux[jb] * area[jb]
+            for b in range(OCEAN_REGIONS):
+                sums[b] = sums[b] + jnp.where(region[jb] == b, product, 0.0)
+        total[...] = jnp.zeros_like(total)
         for b in range(OCEAN_REGIONS):
-            part = lax.dot_general(
-                jnp.ones((ROWS, width), F32),
-                jnp.where(region_all == b, product, 0.0),
-                NT, precision=HIGHEST, preferred_element_type=F32,
-            )
-            fx_rows = jnp.where(iota((ROWS, height), 0) == b, part, fx_rows)
-        fx[...] = jnp.zeros_like(fx)
-        fx[:, pl.ds(0, height)] = fx_rows
-
+            line = jnp.sum(sums[b], axis=0, keepdims=True)
+            for at in range(0, width, 128):
+                piece = line[:, at : at + 128]
+                folded = piece if at == 0 else folded + piece
+            total[pl.ds(b, 1), :] = folded
+
+    flux_total()
+    theta_copy(0).wait()
+    theta_copy(last).wait()
     edge[...] = jnp.zeros_like(edge)
     top[...] = jnp.zeros_like(top)
     for k in range(tiers):
-        edge[pl.ds(k, 1), :] = theta[k, 0, pl.ds(0, 1), :]
-        top[pl.ds(k, 1), :] = theta[k, last, pl.ds(ROWS - 1, 1), :]
+        edge[pl.ds(k, 1), :] = theta[0, k, pl.ds(0, 1), :]
+        top[pl.ds(k, 1), :] = theta[last, k, pl.ds(ROWS - 1, 1), :]
     edge[pl.ds(tiers, 1), :] = depth[0, pl.ds(0, 1), :].astype(F32)
     top[pl.ds(tiers, 1), :] = depth[last, pl.ds(ROWS - 1, 1), :].astype(F32)
-    flux_start()
 
     edge_copy = pltpu.make_async_remote_copy(
         edge, edge_in, edge_sem.at[0], edge_sem.at[1],
@@ -126,8 +160,8 @@
     def first_sends():
         pl.semaphore_wait(barrier, nlon - 1 + nlat - 1)
         edge_copy.start()
-        for step in range(1, nlon):
-            to_lon(fx, fx_in, fx_send, fx_recv, step).start()
+        for step in range(1, nlat):
+            to_lat(step).start()
 
         @pl.when(mylat == nlat - 1)
         def _():
@@ -140,7 +174,7 @@
         deep = depth[jb].astype(F32)
 
         def above(own, k):
-            row = theta[k, jb + 1, pl.ds(0, 1), :] if cap_row is None else cap_row(k)
+            row = theta[jb + 1, k, pl.ds(0, 1), :] if cap_row is None else cap_row(k)
             return jnp.concatenate([own[1:], row], axis=0)
 
         def twice(x, y):
@@ -159,15 +193,16 @@
         warm = jnp.zeros((ROWS, width), F32)
         water = jnp.zeros((ROWS, width), F32)
         kept = []
-        acc = None
+        accs = [None, None]
         for first in range(0, tiers, GROUP):
             tents, picks = [], []
+            side = (first // GROUP) % 2
             for k in range(first, min(first + GROUP, tiers)):
-                th = theta[k, jb]
+                th = theta[jb, k]
                 both = th + above(th, k)
                 face = 0.5 * both
                 volume = jnp.where(wet > float(k), dz[k] * dx, 0.0)
-                moved = volume * speed[k, jb]
+                moved = volume * speed[jb, k]
                 heat = heat + moved * face
                 warm = warm + volume * face
                 water = water + volume
@@ -181,7 +216,7 @@
                 high = jnp.floor(low * (1.0 / DIGIT))
                 digit = low - DIGIT * high
                 high2 = twice(high, high)
-                digit2 = twice(digit, digit - 8.0)
+                digit2 = twice(digit, digit - 8.0) if side == 0 else twice(digit - 8.0, digit)
                 under_h = under.astype(BF).astype(F32)
                 upper_h = upper.astype(BF).astype(F32)
                 under_l, upper_l = under - under_h, upper - upper_h
@@ -212,7 +247,7 @@
                 jnp.concatenate(tents, axis=1), jnp.concatenate(picks, axis=1), NT,
                 preferred_element_type=F32,
             )
-            acc = part if acc is None else acc + part
+            accs[side] = part if accs[side] is None else accs[side] + part
 
         lane = iota((ROWS, 128), 1)
         row = iota((ROWS, 128), 0)
@@ -222,17 +257,21 @@
             return jnp.take_along_axis(x, source, axis=1, mode="promise_in_bounds")
 
         for pair in range(PAIRS):
-            cols = acc[:, 128 * pair : 128 * pair + 128]
+            cols = [x[:, 128 * pair : 128 * pair + 128] for x in accs]
             held = []
             for half in range(2):
                 out = jnp.zeros((ROWS, 128), F32)
                 for n in range(8):
-                    at = 16 * n + 8 * half
-                    one_tent = cols[at : at + ROWS] + cols[128 + at : 128 + at + ROWS]
+                    ats = (16 * n + 8 * half, 16 * n + 8 * (1 - half))
+                    one_tent = tree(
+                        [x[p + at : p + at + ROWS] for x, at in zip(cols, ats) for p in (0, 128)]
+                    )
                     out = jnp.where(lane % 8 == n, align(one_tent, n), out)
                 held.append(out)
-            final = cols[256 : 256 + ROWS] + cols[256 + ROWS :]
-            held[0] = held[0] + jnp.where(lane % 8 == 0, align(final, DIGIT), 0.0)
+            final = tree(
+                [align(x[256 : 256 + ROWS] + x[256 + ROWS :], DIGIT) for x in cols]
+            )
+            held[0] = held[0] + jnp.where(lane % 8 == 0, final, 0.0)
             left = lane % 16 < 8
             buf[jb, pl.ds(2 * pair * ROWS, ROWS), :] = jnp.where(
                 left, held[0], pltpu.roll(held[1], 8, 1)
@@ -241,6 +280,7 @@
                 left, pltpu.roll(held[0], 120, 1), held[1]
             )
         kept = kept + [two_parts(heat), two_parts(warm), two_parts(water)]
+        kept.append(two_parts(flux[jb] * area[jb]))
         nothing = jnp.zeros((ROWS, width), F32)
         basin = []
         for b in range(OCEAN_REGIONS):
@@ -255,6 +295,8 @@
             whole = table[at : at + ROWS] + table[at + ROWS : at + 2 * ROWS]
             line = jnp.where(lane % STRIDE == k, align(whole, k), line)
         buf[jb, pl.ds(OCEAN_REGIONS * ROWS, ROWS), :] = line
+
+    def publish(jb):
         for offset in range(1, nlon):
             share(offset, buf.at[jb], got.at[offset - 1, jb]).start()
 
@@ -281,48 +323,40 @@
             n = top.shape[0]
             cap[...] = found[:n] + found[n : 2 * n] + found[2 * n :]
 
-    def flux_middle():
-        for step in range(1, nlon):
-            to_lon(fx, fx_in, fx_send, fx_recv, step).wait()
-        mine = fx[...]
-        whole = jnp.zeros_like(mine)
-        for owner in range(nlon):
-            piece = mine
-            for step in range(1, nlon):
-                came = lax.rem(mylon + nlon - step, nlon)
-                piece = jnp.where(came == owner, fx_in[step - 1], piece)
-            whole = whole + piece
-        fx[...] = whole
-        total[...] = jnp.broadcast_to(jnp.sum(whole, axis=1, keepdims=True), total.shape)
-        for step in range(1, nlat):
-            to_lat(step).start()
-
-    def flux_end():
+    def southern_flux():
         for step in range(1, nlat):
             to_lat(step).wait()
         before = jnp.zeros(total.shape, F32)
         for step in range(1, nlat):
             before = before + jnp.where(mylat >= step, total_in[step - 1], 0.0)
-        until = (iota((height, height), 0) <= iota((height, height), 1)).astype(F32)
-        run = jnp.dot(
-            fx[:, pl.ds(0, height)], until, precision=HIGHEST, preferred_element_type=F32
-        )
-        out = implied_scale * (before[:, :1] + run)
-        raw[blocks, 0, :, pl.ds(0, height)] = out
-
-    def iteration(it, carry):
-        @pl.when(it == min(4, last - 1))
-        def _():
-            flux_middle()
-
-        compute(it, None)
-        return carry
-
-    first_sends()
-    lax.fori_loop(0, last, iteration, 0)
-    northern_row()
-    compute(last, lambda k: cap[pl.ds(k, 1), :])
-    flux_end()
+        lane = iota((ROWS, 128), 1)
+        line = jnp.zeros((1, 128), F32)
+        for b in range(OCEAN_REGIONS):
+            line = jnp.where(
+                lane[:1] == b * STRIDE + tiers + 4,
+                jnp.sum(before[b : b + 1], axis=1, keepdims=True), line,
+            )
+        at = OCEAN_REGIONS * ROWS
+        buf[last, pl.ds(at, 1), :] = buf[last, pl.ds(at, 1), :] + line
+
+    cuts = [0] + [at for at in CUTS if at < blocks] + [blocks]
+    for segment in range(len(cuts) - 1):
+        members = range(cuts[segment], cuts[segment + 1])
+        final = members[-1] == last
+        for jb in members:
+            speed_copy(jb).wait()
+            if 0 < jb + 1 < last:
+                theta_copy(jb + 1).wait()
+        if final:
+            northern_row()
+        for jb in members:
+            compute(jb, (lambda k: cap[pl.ds(k, 1), :]) if jb == last else None)
+        if segment == 0:
+            first_sends()
+        if final:
+            southern_flux()
+        for jb in members:
+            publish(jb)
     for offset in range(1, nlon):
         share(offset, buf, got.at[offset - 1]).wait()
     for jb in range(blocks):
@@ -330,13 +364,12 @@
         raw[jb] = both.reshape(OCEAN_REGIONS + 1, ROWS, 128)
 
 
-def finish(width_total, raw, class_o, stream_o, heat_o, implied_o):
-    blocks, height = raw.shape[0] - 1, stream_o.shape[2]
+def finish(width_total, height_total, raw, class_o, stream_o, heat_o, implied_o):
+    blocks, height = raw.shape[0], stream_o.shape[2]
     tiers = stream_o.shape[1]
     unit_scale = math.sqrt(THERMAL_BINS / (width_total * tiers))
     for b in range(OCEAN_REGIONS):
         class_o[b] = unit_scale * raw[:blocks, b]
-    implied_o[...] = raw[blocks, 0, :OCEAN_REGIONS, :height]
     table = raw[:blocks, OCEAN_REGIONS].reshape(height, 128)
     dst, src = iota((128, 128), 0), iota((128, 128), 1)
     chain = (src // STRIDE == dst // STRIDE) & (src <= dst) & (src % STRIDE < tiers)
@@ -345,7 +378,7 @@
     )
     for b in range(OCEAN_REGIONS):
         stream_o[b] = stream[b * STRIDE : b * STRIDE + tiers]
-    row, lane = iota((4 * ROWS, 128), 0), iota((4 * ROWS, 128), 1)
+    row, lane = iota((6 * ROWS, 128), 0), iota((6 * ROWS, 128), 1)
     kind, place, slot = row // ROWS, row % ROWS, lane % STRIDE
     own = place == lane // STRIDE
     choose = (
@@ -353,13 +386,22 @@
         | ((kind == 1) & own & (slot < tiers))
         | ((kind == 2) & (slot == tiers + 1))
         | ((kind == 3) & (slot == tiers + 2))
+        | ((kind == 4) & own & (slot == tiers + 3))
+        | ((kind == 5) & own & (slot == tiers + 4))
     )
     rows = lax.dot_general(
         choose.astype(F32), table, NT, precision=HIGHEST, preferred_element_type=F32
     )
-    mean = rows[2 * ROWS : 3 * ROWS] / rows[3 * ROWS :]
+    mean = rows[2 * ROWS : 3 * ROWS] / rows[3 * ROWS : 4 * ROWS]
     heat = (unit_scale / 16.0) * (rows[:ROWS] - rows[ROWS : 2 * ROWS] * mean)
     heat_o[...] = heat[:OCEAN_REGIONS]
+    until = (iota((height, height), 0) <= iota((height, height), 1)).astype(F32)
+    run = jnp.dot(
+        rows[4 * ROWS : 5 * ROWS], until, precision=HIGHEST, preferred_element_type=F32
+    )
+    before = jnp.sum(rows[5 * ROWS :], axis=1, keepdims=True)
+    implied = (2.0 / math.sqrt(width_total * height_total)) * (before + run)
+    implied_o[...] = implied[:OCEAN_REGIONS]
 
 
 def body(speed, theta, dz, dx, area, flux, depth, region, seam):
@@ -367,31 +409,38 @@
     nlon, nlat = lax.axis_size("lon"), lax.axis_size("lat")
     blocks = height // ROWS
     edge_rows = -(-(tiers + 1) // 8) * 8
-    pad = -(-height // 128) * 128
     flat = (blocks, ROWS, width)
+    any_spec = pl.BlockSpec(memory_space=pltpu.HBM)
     vmem = pl.BlockSpec(memory_space=pltpu.VMEM)
     dma = pltpu.SemaphoreType.DMA
     raw = pl.pallas_call(
-        functools.partial(kernel, nlon, nlat, width * nlon, height * nlat),
+        functools.partial(kernel, nlon, nlat),
         name="transport",
-        out_shape=jax.ShapeDtypeStruct((blocks + 1, OCEAN_REGIONS + 1, ROWS, pad), F32),
-        in_specs=[pl.BlockSpec(memory_space=pltpu.SMEM)] + [vmem] * 8,
+        out_shape=pltpu.VMEM((blocks, OCEAN_REGIONS + 1, ROWS, 128), F32),
+        in_specs=[any_spec] * 9,
         out_specs=vmem,
         scratch_shapes=[
+            pltpu.SMEM((tiers,), F32),
+            pltpu.VMEM((blocks, tiers, ROWS, width), F32),
+            pltpu.VMEM((blocks, tiers, ROWS, width), F32),
+            pltpu.VMEM(flat, F32),
+            pltpu.VMEM(flat, F32),
+            pltpu.VMEM(flat, F32),
+            pltpu.VMEM(flat, jnp.int32),
+            pltpu.VMEM(flat, jnp.int32),
+            pltpu.VMEM((1, width), jnp.int32),
             pltpu.VMEM((edge_rows, width), F32),
             pltpu.VMEM((edge_rows, width), F32),
             pltpu.VMEM((edge_rows, width), F32),
             pltpu.VMEM((nlon - 1, edge_rows, width), F32),
             pltpu.VMEM((edge_rows, width), F32),
-            pltpu.VMEM((ROWS, pad), F32),
-            pltpu.VMEM((nlon - 1, ROWS, pad), F32),
             pltpu.VMEM((ROWS, 128), F32),
             pltpu.VMEM((nlat - 1, ROWS, 128), F32),
             pltpu.VMEM((blocks, 5 * ROWS, 128), F32),
             pltpu.VMEM((nlon - 1, blocks, 5 * ROWS, 128), F32),
+            dma((2, blocks)),
+            dma((7,)),
             dma((2,)),
-            dma((nlon - 1,)),
-            dma((nlon - 1,)),
             dma((nlon - 1,)),
             dma((nlon - 1,)),
             dma((nlat - 1,)),
@@ -403,18 +452,23 @@
             collective_id=0, has_side_effects=True, vmem_limit_bytes=40 << 20
         ),
     )(
-        dz,
-        speed.reshape(tiers, *flat),
-        theta.reshape(tiers, *flat),
-        dx.reshape(flat),
-        area.reshape(flat),
-        flux.reshape(flat),
-        depth.reshape(flat),
-        region.reshape(flat),
-        seam.reshape(1, width),
+        *[
+            pltpu.with_memory_space_constraint(x, pltpu.HBM)
+            for x in (
+                dz,
+                speed.reshape(tiers, *flat),
+                theta.reshape(tiers, *flat),
+                dx.reshape(flat),
+                area.reshape(flat),
+                flux.reshape(flat),
+                depth.reshape(flat),
+                region.reshape(flat),
+                seam.reshape(1, width),
+            )
+        ]
     )
     out = pl.pallas_call(
-        functools.partial(finish, width * nlon),
+        functools.partial(finish, width * nlon, height * nlat),
         name="finish",
         out_shape=(
             jax.ShapeDtypeStruct((OCEAN_REGIONS, blocks, ROWS, THERMAL_BINS), F32),

time: 27.9 us -> 17.8 us (0.64); the launches traced: 27.5 us -> 17.7 us
  local copies, waits for them, and re-layouts: 7.31 us -> 0 us
  Pallas kernels: 19.5 us -> 17 us
    unnamed x18 -> x0, local copies, waits for them, and re-layouts: 7.31 us -> none
    pallas_call x2, Pallas kernels: 19.5 us -> 17 us  [the longest x1 16.1 us: body(): pl.pallas_call(functools.partial(kernel, nlon, nlat), name='transport', o...]
where the time goes in v2:
time: 17.8 us; the launch traced here: 17.7 us
  Pallas kernels  17 us (96%)
  between operations  0.64 us (4%)
    pallas_call x1, Pallas kernels, body(): pl.pallas_call(functools.partial(kernel, nlon, nlat), name='transport', o...  16.1 us
    pallas_call x1, Pallas kernels, body(): pl.pallas_call(functools.partial(finish, width * nlon, height * nlat), na...  0.94 us

profile of v2, /device:TPU:0, one launch (start us, length us, event | category | flops | bytes accessed | tf_op | source)
XLA Modules:
  0.0 17.7 jit_solution(7057801528423107207)
XLA Ops:
  0.6 16.1 %transport.1.raw = f32[8,5,8,128]{3,2,1,0:T(8,128)S(1)} custom-call(f32[16]{0:T(128)} %dz_h.1, f32[16,8,8,256]{3,2,1,0:T(8,128)} %bitcast.10, f32[16,8,8,256]{3,2,1,0:T(8,128)} %bitcast.11, f32[8,8,256]{2,1,0:T(8,128)} %bitcast.12, f32[8,8,256]{2,1,0:T(8,128)} %bitcast.13, f32[8,8,256]{2,1,0:T(8,128)} %bitcast.14, s32[8,8,256]{2,1,0:T(8,128)} %bitcast.15, ...), custom_call_target="tpu_custom_call" | custom-call | tf_op jit(solution)/shard_map/transport/pallas_call | solution.py:416
  16.7 0.9 %finish.1 = (f32[4,8,8,128]{3,2,1,0:T(8,128)}, f32[4,16,64]{2,1,0:T(8,128)}, f32[4,64]{1,0:T(4,128)}, f32[4,64]{1,0:T(4,128)}) custom-call(f32[8,5,8,128]{3,2,1,0:T(8,128)S(1)} %transport.1.raw), custom_call_target="tpu_custom_call" | custom-call | tf_op jit(solution)/shard_map/finish/pallas_call | solution.py:470

commit v3 on v2

--- a/solution.py
+++ b/solution.py
@@ -19,7 +19,8 @@
 PAIRS = OCEAN_REGIONS // 2
 GROUP = 4
 STRIDE = 32
-CUTS = (2, 4, 6)
+EARLY = 2
+LATE = 1
 MESH = pl.DeviceIdType.MESH
 NT = (((1,), (1,)), ((), ()))
 HIGHEST = lax.Precision.HIGHEST
@@ -102,13 +103,15 @@
             product = flux[jb] * area[jb]
             for b in range(OCEAN_REGIONS):
                 sums[b] = sums[b] + jnp.where(region[jb] == b, product, 0.0)
-        total[...] = jnp.zeros_like(total)
+        lane = iota((1, 128), 1)
+        line = jnp.zeros((1, 128), F32)
         for b in range(OCEAN_REGIONS):
-            line = jnp.sum(sums[b], axis=0, keepdims=True)
-            for at in range(0, width, 128):
-                piece = line[:, at : at + 128]
-                folded = piece if at == 0 else folded + piece
-            total[pl.ds(b, 1), :] = folded
+            line = jnp.where(
+                lane == b * STRIDE + tiers + 4,
+                jnp.sum(jnp.sum(sums[b], axis=0, keepdims=True), axis=1, keepdims=True),
+                line,
+            )
+        total[...] = line
 
     flux_total()
     theta_copy(0).wait()
@@ -159,16 +162,16 @@
 
     def first_sends():
         pl.semaphore_wait(barrier, nlon - 1 + nlat - 1)
-        edge_copy.start()
         for step in range(1, nlat):
             to_lat(step).start()
+        edge_copy.start()
 
         @pl.when(mylat == nlat - 1)
         def _():
             for step in range(1, nlon):
                 to_lon(top, top_in, top_send, top_recv, step).start()
 
-    def compute(jb, cap_row):
+    def main(jb, cap_row):
         reg = region[jb].astype(F32)
         dx = dx_all[jb]
         deep = depth[jb].astype(F32)
@@ -249,6 +252,19 @@
             )
             accs[side] = part if accs[side] is None else accs[side] + part
 
+        kept = kept + [two_parts(heat), two_parts(warm), two_parts(water)]
+        kept.append(two_parts(flux[jb] * area[jb]))
+        nothing = jnp.zeros((ROWS, width), F32)
+        basin = []
+        for b in range(OCEAN_REGIONS):
+            basin += [twice(jnp.where(reg == float(b), 1.0, 0.0), nothing), zero]
+        table = lax.dot_general(
+            jnp.concatenate(kept, axis=0), jnp.concatenate(basin, axis=0), NT,
+            preferred_element_type=F32,
+        )
+        return accs, table
+
+    def tail(jb, accs, table):
         lane = iota((ROWS, 128), 1)
         row = iota((ROWS, 128), 0)
 
@@ -279,84 +295,94 @@
             buf[jb, pl.ds((2 * pair + 1) * ROWS, ROWS), :] = jnp.where(
                 left, pltpu.roll(held[0], 120, 1), held[1]
             )
-        kept = kept + [two_parts(heat), two_parts(warm), two_parts(water)]
-        kept.append(two_parts(flux[jb] * area[jb]))
-        nothing = jnp.zeros((ROWS, width), F32)
-        basin = []
-        for b in range(OCEAN_REGIONS):
-            basin += [twice(jnp.where(reg == float(b), 1.0, 0.0), nothing), zero]
-        table = lax.dot_general(
-            jnp.concatenate(kept, axis=0), jnp.concatenate(basin, axis=0), NT,
-            preferred_element_type=F32,
-        )
         line = jnp.zeros((ROWS, 128), F32)
-        for k in range(len(kept)):
+        for k in range(table.shape[0] // (2 * ROWS)):
             at = 2 * ROWS * k
             whole = table[at : at + ROWS] + table[at + ROWS : at + 2 * ROWS]
             line = jnp.where(lane % STRIDE == k, align(whole, k), line)
         buf[jb, pl.ds(OCEAN_REGIONS * ROWS, ROWS), :] = line
 
     def publish(jb):
-        for offset in range(1, nlon):
+        for offset in range(nlon - 1, 0, -1):
             share(offset, buf.at[jb], got.at[offset - 1, jb]).start()
 
-    def northern_row():
+    def await_north():
         edge_copy.wait()
-
-        @pl.when(mylat < nlat - 1)
-        def _():
-            cap[...] = edge_in[...]
 
         @pl.when(mylat == nlat - 1)
         def _():
-            found = jnp.zeros((3 * top.shape[0], width), F32)
-            for step in range(nlon):
-                if step:
-                    to_lon(top, top_in, top_send, top_recv, step).wait()
-                block = top_in[step - 1] if step else top[...]
-                owner = lax.rem(mylon + nlon - step, nlon)
-                here = iota((width, width), 0) + owner * width == seam[...]
-                found = found + jnp.dot(
+            for step in range(1, nlon):
+                to_lon(top, top_in, top_send, top_recv, step).wait()
+
+    def northern_row():
+        n = top.shape[0]
+        folded = []
+        for step in range(nlon):
+            block = top_in[step - 1] if step else top[...]
+            owner = lax.rem(mylon + nlon - step, nlon)
+            here = iota((width, width), 0) == seam[...] - owner * width
+            folded.append(
+                jnp.dot(
                     exact_parts(block), jnp.where(here, 1.0, 0.0).astype(BF),
                     preferred_element_type=F32,
                 )
-            n = top.shape[0]
-            cap[...] = found[:n] + found[n : 2 * n] + found[2 * n :]
+            )
+        found = sum(folded[1:], folded[0])
+        row = found[:n] + found[n : 2 * n] + found[2 * n :]
+        return jnp.where(mylat == nlat - 1, row, edge_in[...])
 
     def southern_flux():
         for step in range(1, nlat):
             to_lat(step).wait()
-        before = jnp.zeros(total.shape, F32)
+        line = jnp.zeros(total.shape, F32)
         for step in range(1, nlat):
-            before = before + jnp.where(mylat >= step, total_in[step - 1], 0.0)
-        lane = iota((ROWS, 128), 1)
-        line = jnp.zeros((1, 128), F32)
-        for b in range(OCEAN_REGIONS):
-            line = jnp.where(
-                lane[:1] == b * STRIDE + tiers + 4,
-                jnp.sum(before[b : b + 1], axis=1, keepdims=True), line,
-            )
+            line = line + jnp.where(mylat >= step, total_in[step - 1], 0.0)
         at = OCEAN_REGIONS * ROWS
         buf[last, pl.ds(at, 1), :] = buf[last, pl.ds(at, 1), :] + line
 
-    cuts = [0] + [at for at in CUTS if at < blocks] + [blocks]
-    for segment in range(len(cuts) - 1):
-        members = range(cuts[segment], cuts[segment + 1])
-        final = members[-1] == last
+    def loaded(members):
         for jb in members:
             speed_copy(jb).wait()
             if 0 < jb + 1 < last:
                 theta_copy(jb + 1).wait()
-        if final:
-            northern_row()
-        for jb in members:
-            compute(jb, (lambda k: cap[pl.ds(k, 1), :]) if jb == last else None)
-        if segment == 0:
-            first_sends()
-        if final:
-            southern_flux()
-        for jb in members:
-            publish(jb)
+
+    def capped(jb):
+        return (lambda k: cap[pl.ds(k, 1), :]) if jb == last else None
+
+    early, late = min(EARLY, last), max(blocks - LATE, min(EARLY, last))
+    loaded(range(early))
+    pending = []
+    for jb in range(early):
+        pending.append((jb, main(jb, None)))
+    for jb, made in pending:
+        tail(jb, *made)
+    loaded(range(early, blocks))
+    first_sends()
+    for jb in range(early):
+        publish(jb)
+    ahead = None
+    for jb in range(early, late):
+        made = main(jb, None)
+        if ahead is not None:
+            tail(*ahead)
+            publish(ahead[0])
+        ahead = (jb, *made)
+    if ahead is not None:
+        tail(*ahead)
+    await_north()
+    if ahead is not None:
+        publish(ahead[0])
+    cap[...] = northern_row()
+    ahead = None
+    for jb in range(late, blocks):
+        made = main(jb, capped(jb))
+        if ahead is not None:
+            tail(*ahead)
+            publish(ahead[0])
+        ahead = (jb, *made)
+    tail(*ahead)
+    southern_flux()
+    publish(last)
     for offset in range(1, nlon):
         share(offset, buf, got.at[offset - 1]).wait()
     for jb in range(blocks):
@@ -434,8 +460,8 @@
             pltpu.VMEM((edge_rows, width), F32),
             pltpu.VMEM((nlon - 1, edge_rows, width), F32),
             pltpu.VMEM((edge_rows, width), F32),
-            pltpu.VMEM((ROWS, 128), F32),
-            pltpu.VMEM((nlat - 1, ROWS, 128), F32),
+            pltpu.VMEM((1, 128), F32),
+            pltpu.VMEM((nlat - 1, 1, 128), F32),
             pltpu.VMEM((blocks, 5 * ROWS, 128), F32),
             pltpu.VMEM((nlon - 1, blocks, 5 * ROWS, 128), F32),
             dma((2, blocks)),

time: 17.8 us -> 17.6 us (0.989)
  Pallas kernels: 17 us -> 16.8 us
    pallas_call x1, Pallas kernels: 16.1 us -> 15.9 us  [body(): pl.pallas_call(functools.partial(kernel, nlon, nlat), name='transport', o...]
where the time goes in v3:
time: 17.6 us; the launch traced here: 17.5 us
  Pallas kernels  16.8 us (95%)
  between operations  0.64 us (4%)
    pallas_call x1, Pallas kernels, body(): pl.pallas_call(functools.partial(kernel, nlon, nlat), name='transport', o...  15.9 us
    pallas_call x1, Pallas kernels, body(): pl.pallas_call(functools.partial(finish, width * nlon, height * nlat), na...  0.94 us

profile of v3, /device:TPU:0, one launch (start us, length us, event | category | flops | bytes accessed | tf_op | source)
XLA Modules:
  0.0 17.5 jit_solution(3901702822256778408)
XLA Ops:
  0.6 15.9 %transport.1.raw = f32[8,5,8,128]{3,2,1,0:T(8,128)S(1)} custom-call(f32[16]{0:T(128)} %dz_h.1, f32[16,8,8,256]{3,2,1,0:T(8,128)} %bitcast.10, f32[16,8,8,256]{3,2,1,0:T(8,128)} %bitcast.11, f32[8,8,256]{2,1,0:T(8,128)} %bitcast.12, f32[8,8,256]{2,1,0:T(8,128)} %bitcast.13, f32[8,8,256]{2,1,0:T(8,128)} %bitcast.14, s32[8,8,256]{2,1,0:T(8,128)} %bitcast.15, ...), custom_call_target="tpu_custom_call" | custom-call | tf_op jit(solution)/shard_map/transport/pallas_call | solution.py:442
  16.5 0.9 %finish.1 = (f32[4,8,8,128]{3,2,1,0:T(8,128)}, f32[4,16,64]{2,1,0:T(8,128)}, f32[4,64]{1,0:T(4,128)}, f32[4,64]{1,0:T(4,128)}) custom-call(f32[8,5,8,128]{3,2,1,0:T(8,128)S(1)} %transport.1.raw), custom_call_target="tpu_custom_call" | custom-call | tf_op jit(solution)/shard_map/finish/pallas_call | solution.py:496
